TPU v7x, 32 devices: a whole 2x2x4 slice. The times are simulated.
32 devices in a mesh: expert: 4 (over x, core), shard: 8 (over z, y).
Axes of the slice: x: 2, y: 2, z: 4, core: 2. Of those that a mesh axis runs over, the one named last changes fastest.
Arguments:
- master_gate: float32 [64, 2048, 1024], P('expert', 'shard'), may hold values from -0.1875 to 0.1875
- second_gate: bfloat16 [64, 2048, 1024], P('expert', 'shard'), may hold values from -0.0625 to 0.0625
- master_up: float32 [64, 2048, 1024], P('expert', 'shard'), may hold values from -0.1875 to 0.1875
- second_up: bfloat16 [64, 2048, 1024], P('expert', 'shard'), may hold values from -0.0625 to 0.0625
- master_down: float32 [64, 1024, 2048], P('expert', None, 'shard'), may hold values from -0.25 to 0.25
- second_down: bfloat16 [64, 1024, 2048], P('expert', None, 'shard'), may hold values from -0.09375 to 0.09375
- router_weight: float32 [2048, 64], P('shard', 'expert'), may hold values from -0.125 to 0.125
- router_gain: float32 [2048], P('shard'), may hold values from 0.25 to 1.75
Outputs:
- final_gate: bfloat16 [64, 2048, 1024], P('expert', None, 'shard')
- final_up: bfloat16 [64, 2048, 1024], P('expert', None, 'shard')
- final_down: bfloat16 [64, 1024, 2048], P('expert', 'shard')
- scale_gate: float32 [64, 1024], P('expert', 'shard')
- scale_up: float32 [64, 1024], P('expert', 'shard')
- scale_down: float32 [64, 1024], P('expert', 'shard')
- serve_router: bfloat16 [2048, 64], replicated
All inputs are finite; a program needn't handle non-finite values. Where the computation divides by a largest or mean magnitude, that divisor is 1e-20 or more.
Results may differ from a plain program's by a relative error of at most 0.001.
Values may be sent and summed in bfloat16 or wider, within the bound.
A program may use at most 192 MiB of HBM per device.

v0:
```python
import jax
import jax.numpy as jnp
from jax import lax
from jax.sharding import PartitionSpec as P


def per_device(
    master_gate,
    second_gate,
    master_up,
    second_up,
    master_down,
    second_down,
    router_weight,
    router_gain,
):
    merged_gate = master_gate + second_gate.astype(jnp.float32)
    merged_up = master_up + second_up.astype(jnp.float32)
    merged_down = master_down + second_down.astype(jnp.float32)
    scale_gate, scale_up, scale_down = lax.pmax(
        (
            jnp.max(jnp.abs(merged_gate), axis=1),
            jnp.max(jnp.abs(merged_up), axis=1),
            jnp.max(jnp.abs(merged_down), axis=2),
        ),
        "shard",
    )
    narrow_gate, narrow_up, narrow_down = (
        (merged_gate / jnp.expand_dims(scale_gate, 1)).astype(jnp.bfloat16),
        (merged_up / jnp.expand_dims(scale_up, 1)).astype(jnp.bfloat16),
        (merged_down / jnp.expand_dims(scale_down, 2)).astype(jnp.bfloat16),
    )
    final_gate, final_up = (
        lax.all_to_all(narrow_gate, "shard", split_axis=2, concat_axis=1, tiled=True),
        lax.all_to_all(narrow_up, "shard", split_axis=2, concat_axis=1, tiled=True),
    )
    final_down = lax.all_to_all(narrow_down, "shard", split_axis=1, concat_axis=2, tiled=True)
    scale_gate = lax.dynamic_slice_in_dim(
        scale_gate, lax.axis_index("shard") * final_gate.shape[2], final_gate.shape[2], axis=1
    )
    scale_up = lax.dynamic_slice_in_dim(
        scale_up, lax.axis_index("shard") * final_up.shape[2], final_up.shape[2], axis=1
    )
    scale_down = lax.dynamic_slice_in_dim(
        scale_down, lax.axis_index("shard") * final_down.shape[1], final_down.shape[1], axis=1
    )
    part_router = (router_weight * router_gain[:, None]).astype(jnp.bfloat16)
    row_router = lax.all_gather(part_router, "shard", axis=0, tiled=True)
    serve_router = lax.all_gather(row_router, "expert", axis=1, tiled=True)
    return (final_gate, final_up, final_down, scale_gate, scale_up, scale_down, serve_router)


def solution(mesh):
    in_specs = (
        P("expert", "shard", None),
        P("expert", "shard", None),
        P("expert", "shard", None),
        P("expert", "shard", None),
        P("expert", None, "shard"),
        P("expert", None, "shard"),
        P("shard", "expert"),
        P("shard"),
    )
    out_specs = (
        P("expert", None, "shard"),
        P("expert", None, "shard"),
        P("expert", "shard", None),
        P("expert", "shard"),
        P("expert", "shard"),
        P("expert", "shard"),
        P(),
    )
    return jax.shard_map(
        per_device, mesh=mesh, in_specs=in_specs, out_specs=out_specs, check_vma=False
    )
```

profile of v0, /device:TPU:0, one launch (start us, length us, event | category | flops | bytes accessed | tf_op | source)
XLA Modules:
  0.0 877.2 jit_solution(5564650451525219035)
XLA Ops:
  7.2 0.0 all-reduce.3.cloned.1.call-start
  7.2 17.6 %copy.34 = f32[16,256,1024]{1,0,2:T(8,128)} copy(f32[16,256,1024]{2,1,0:T(8,128)} %param.10) | data formatting | bytes 33554432 | tf_op args[2]
  24.8 12.5 %copy.33 = bf16[16,256,1024]{1,0,2:T(8,128)(2,1)} copy(bf16[16,256,1024]{2,1,0:T(8,128)(2,1)} %param.11) | data formatting | bytes 16777216 | tf_op args[3]
  37.3 17.6 %copy.31 = f32[16,256,1024]{1,0,2:T(8,128)} copy(f32[16,256,1024]{2,1,0:T(8,128)} %param.8) | data formatting | bytes 33554432 | tf_op args[0]
  54.9 12.5 %copy.30 = bf16[16,256,1024]{1,0,2:T(8,128)(2,1)} copy(bf16[16,256,1024]{2,1,0:T(8,128)(2,1)} %param.9) | data formatting | bytes 16777216 | tf_op args[1]
  67.4 0.0 copy-start
  67.4 0.0 copy-start.1
  67.4 0.0 slice-start
  67.4 11.1 %abs_reduce_fusion.1 = f32[16,1024]{0,1:T(8,128)} fusion(f32[16,256,1024]{1,0,2:T(8,128)} %copy.34, bf16[16,256,1024]{1,0,2:T(8,128)(2,1)} %copy.33), kind=kLoop, calls=%fused_computation.4 | loop fusion | flops 16760832 | bytes 25231360 | tf_op jit(solution)/shard_map/reduce_max | solution.py:23
  78.5 2.1 copy-done
  80.6 2.4 copy-done.1
  83.0 0.0 slice-start.1
  83.0 4.3 abs_reduce_fusion.2
  87.3 0.0 slice-done
  87.3 0.0 slice-done.1
  87.3 29.3 %abs_reduce_fusion = f32[16,1024]{0,1:T(8,128)} fusion(f32[16,1024,256]{2,1,0:T(8,128)} %param.12, bf16[16,1024,256]{2,1,0:T(8,128)(2,1)S(1)} %bitcast.14), kind=kLoop, calls=%fused_computation.2 | loop fusion | flops 16760832 | bytes 25231360 | tf_op jit(solution)/shard_map/reduce_max | solution.py:24
  116.5 0.0 all-reduce.3.cloned.1.call-update
  116.6 92.5 %all-reduce.3.cloned.1.call-done = (f32[16,1024]{0,1:T(8,128)}, f32[16,1024]{0,1:T(8,128)}, f32[16,1024]{0,1:T(8,128)}) async-done(((f32[16,1024]{0,1:T(8,128)}, f32[16,1024]{0,1:T(8,128)}, f32[16,1024]{0,1:T(8,128)}), (f32[16,1024]{0,1:T(8,128)}, f32[16,1024]{0,1:T(8,128)}, f32[16,1024]{0,1:T(8,128)})) %all-reduce.3.cloned.1.call-update) | async-done | bytes 196624 | tf_op jit(solution)/shard_map/pmax | solution.py:20
  209.0 20.5 %divide_convert_fusion.1 = (bf16[16,256,1024]{1,0,2:T(8,128)(2,1)}, bf16[16,256,1024]{1,0,2:T(8,128)(2,1)S(1)}) fusion(f32[16,256,1024]{1,0,2:T(8,128)} %copy.34, bf16[16,256,1024]{1,0,2:T(8,128)(2,1)} %copy.33, f32[16,1024]{0,1:T(8,128)} %get-tuple-element.15, f32[16,1024]{0,1:T(8,128)} %get-tuple-element.14, f32[16,256,1024]{1,0,2:T(8,128)} %copy.31, ...), kind=kLoop, calls=%fused_computation.3 | loop fusion | flops 33554432 | bytes 67239936 | tf_op jit(solution)/shard_map/convert_element_type | solution.py:30
  229.6 0.0 copy-start.2
  229.6 187.0 %all_to_all.54 = bf16[16,256,1024]{1,0,2:T(8,128)(2,1)} all-to-all(bf16[16,256,1024]{1,0,2:T(8,128)(2,1)S(1)} %get-tuple-element.18), channel_id=1, replica_groups=mesh['expert'=4,'shard'=8] {'shard'}, dimensions={2} | all-to-all | bytes 16777216 | tf_op jit(solution)/shard_map/all_to_all | solution.py:34
  416.6 4.9 all-to-all-start.1
  421.5 0.0 copy-done.2
  421.5 23.8 %divide_convert_fusion = bf16[16,1024,256]{2,0,1:T(8,128)(2,1)} fusion(f32[16,1024,256]{2,1,0:T(8,128)} %param.12, f32[16,1024]{0,1:T(8,128)S(1)} %copy-done.2, bf16[16,1024,256]{2,1,0:T(8,128)(2,1)} %param.13), kind=kLoop, calls=%fused_computation.1 | loop fusion | flops 16777216 | bytes 33619968 | tf_op jit(solution)/shard_map/convert_element_type | solution.py:31
  445.3 0.0 copy-start.3
  445.3 0.0 copy-start.4
  445.3 158.3 %all-to-all-done.1 = bf16[16,256,1024]{1,0,2:T(8,128)(2,1)} async-done(((bf16[16,256,1024]{1,0,2:T(8,128)(2,1)}), bf16[16,256,1024]{1,0,2:T(8,128)(2,1)}, u32[]{:S(2)}, u32[]{:S(2)}) %all-to-all-start.1) | async-done | bytes 8388640 | tf_op jit(solution)/shard_map/all_to_all | solution.py:35
  603.6 5.0 all-to-all-start.2
  608.6 0.0 copy-done.3
  608.6 0.0 copy-done.4
  608.7 201.9 %all_gather.6 = bf16[2048,16]{0,1:T(8,128)(2,1)S(1)} all-gather(bf16[256,16]{0,1:T(8,128)(2,1)S(1)} %multiply_convert_fusion), channel_id=1, replica_groups=mesh['expert'=4,'shard'=8] {'shard'}, dimensions={0}, use_global_device_ids=true | all-gather | bytes 73728 | tf_op jit(solution)/shard_map/all_gather | solution.py:48
  810.6 6.0 all_gather.7
  816.5 0.8 constant_dynamic-slice_fusion
  817.4 0.7 copy.40
  818.1 0.7 copy.41
  818.7 0.8 constant_dynamic-slice_fusion.2
  819.6 0.7 copy.39
  820.2 12.3 %copy.32 = bf16[16,8,256,128]{3,2,1,0:T(8,128)(2,1)} copy(bf16[16,8,256,128]{2,0,3,1:T(8,128)(2,1)} %bitcast.15) | data formatting | bytes 16777216 | tf_op jit(solution)/shard_map/all_to_all | solution.py:34
  832.5 12.3 %copy.35 = bf16[16,8,256,128]{3,2,1,0:T(8,128)(2,1)} copy(bf16[16,8,256,128]{2,0,3,1:T(8,128)(2,1)} %bitcast.4) | data formatting | bytes 16777216 | tf_op jit(solution)/shard_map/all_to_all | solution.py:35
  844.8 0.0 all-to-all-done.2
  844.8 11.4 %copy.38 = bf16[16,128,8,256]{3,2,1,0:T(8,128)(2,1)} copy(bf16[16,128,8,256]{3,0,1,2:T(8,128)(2,1)} %bitcast.7) | data formatting | bytes 16777216 | tf_op jit(solution)/shard_map/all_to_all | solution.py:37
  856.2 13.4 %all_to_all.50 = bf16[16,128,2048]{2,1,0:T(8,128)(2,1)} reshape(bf16[16,128,8,256]{3,2,1,0:T(8,128)(2,1)} %copy.38) | data formatting | bytes 16777216 | tf_op jit(solution)/shard_map/all_to_all | solution.py:37
  869.6 0.7 copy.53
  (2 shorter events, 0.0 us)
Async XLA Ops:
  7.2 201.8 %all-reduce.3.cloned.1.call-start = ((), (), s32[]{:S(2)}) async-start(), calls=%async_computation.3 | async-start | bytes 3145728 | tf_op jit(solution)/shard_map/pmax | solution.py:20
  67.4 13.2 %copy-start = (f32[16,256,1024]{1,0,2:T(8,128)S(1)}, f32[16,256,1024]{1,0,2:T(8,128)}, u32[]{:S(2)}) copy-start(f32[16,256,1024]{1,0,2:T(8,128)} %copy.31) | copy-start | bytes 50331652
  67.4 15.6 %copy-start.1 = (bf16[16,256,1024]{1,0,2:T(8,128)(2,1)S(1)}, bf16[16,256,1024]{1,0,2:T(8,128)(2,1)}, u32[]{:S(2)}) copy-start(bf16[16,256,1024]{1,0,2:T(8,128)(2,1)} %copy.30) | copy-start | bytes 25165828
  67.4 19.9 %slice-start = ((s8[8388608]{0:T(1024)(128)(4,1)}), s8[4194304]{0:T(1024)(128)(4,1)S(1)}, s32[]{:S(2)}) async-start(s8[8388608]{0:T(1024)(128)(4,1)} %bitcast.13), calls=%async_computation.4 | async-start | bytes 8388608
  83.0 4.3 slice-start.1
  229.6 192.0 %copy-start.2 = (f32[16,1024]{0,1:T(8,128)S(1)}, f32[16,1024]{0,1:T(8,128)}, u32[]{:S(2)}) copy-start(f32[16,1024]{0,1:T(8,128)} %get-tuple-element.16) | copy-start | bytes 196612
  416.6 187.0 %all-to-all-start.1 = ((bf16[16,256,1024]{1,0,2:T(8,128)(2,1)}), bf16[16,256,1024]{1,0,2:T(8,128)(2,1)}, u32[]{:S(2)}, u32[]{:S(2)}) async-start(bf16[16,256,1024]{1,0,2:T(8,128)(2,1)} %get-tuple-element.17), calls=%async_computation.1 | async-start | bytes 16777216 | tf_op jit(solution)/shard_map/all_to_all | solution.py:35
  445.3 163.3 %copy-start.3 = (f32[256,16]{0,1:T(8,128)S(1)}, f32[256,16]{0,1:T(8,128)}, u32[]{:S(2)}) copy-start(f32[256,16]{0,1:T(8,128)} %param.14) | copy-start | bytes 49156
  445.3 163.3 %copy-start.4 = (f32[256]{0:T(256)S(1)}, f32[256]{0:T(256)}, u32[]{:S(2)}) copy-start(f32[256]{0:T(256)} %param.15) | copy-start | bytes 3076
  603.6 241.2 %all-to-all-start.2 = ((bf16[16,1024,256]{2,0,1:T(8,128)(2,1)}), bf16[16,1024,256]{2,0,1:T(8,128)(2,1)}, u32[]{:S(2)}, u32[]{:S(2)}) async-start(bf16[16,1024,256]{2,0,1:T(8,128)(2,1)} %divide_convert_fusion), calls=%async_computation.2 | async-start | bytes 16777216 | tf_op jit(solution)/shard_map/all_to_all | solution.py:37
Sparse Core Ops, SparseCore 0:
  116.7 92.2 all-reduce.2
where the time goes:
time: 880 us; the launch traced here: 877 us
  blocking collectives  395 us (45%)
  waiting for transfers between devices  251 us (29%)
  local copies, waits for them, and re-layouts  118 us (13%)
  other arithmetic  88.9 us (10%)
  between operations  14.1 us (2%)
  starting transfers between devices  10 us (1%)
    all_gather x1, blocking collectives, per_device(): row_router = lax.all_gather(part_router, 'shard', axis=0, tiled=True)  202 us
    all_to_all x1, blocking collectives, per_device(): lax.all_to_all(narrow_gate, 'shard', split_axis=2, concat_axis=1, tiled=T...  187 us
    all_to_all x1, waiting for transfers between devices, per_device(): lax.all_to_all(narrow_up, 'shard', split_axis=2, concat_axis=1, tiled=True)  158 us
    pmax x1, waiting for transfers between devices, per_device(): lax.pmax((jnp.max(jnp.abs(merged_gate), axis=1), jnp.max(jnp.abs(merged_u...  92.5 us
    unnamed x22, local copies, waits for them, and re-layouts  67.4 us
    reduce_max x1, other arithmetic, per_device(): jnp.max(jnp.abs(merged_down), axis=2)  29.3 us
    all_to_all x2, local copies, waits for them, and re-layouts, per_device(): lax.all_to_all(narrow_down, 'shard', split_axis=1, concat_axis=2, tiled=T...  24.8 us
    convert_element_type x1, other arithmetic, per_device(): (merged_down / jnp.expand_dims(scale_down, 2)).astype(jnp.bfloat16)  23.8 us
  transfers between devices with their start and end apart: 3, of which 2 were waited for; matrix products, arithmetic and copies ran while one was open for 6% of the time, Pallas kernels for 0%

commit v1 on v0

--- a/solution.py
+++ b/solution.py
@@ -2,6 +2,14 @@
 import jax.numpy as jnp
 from jax import lax
 from jax.sharding import PartitionSpec as P
+
+
+def write_slabs_by_axis(s0, shard_axis):
+    arr_out = lax.axis_size(shard_axis)
+    z = jnp.split(s0, arr_out, axis=2)
+    e_next = jnp.stack(z)
+    y2 = lax.all_to_all(e_next, axis_name=shard_axis, split_axis=0, concat_axis=0)
+    return jnp.concatenate(y2, axis=1)
 
 
 def per_device(
@@ -31,7 +39,7 @@
         (merged_down / jnp.expand_dims(scale_down, 2)).astype(jnp.bfloat16),
     )
     final_gate, final_up = (
-        lax.all_to_all(narrow_gate, "shard", split_axis=2, concat_axis=1, tiled=True),
+        write_slabs_by_axis(narrow_gate, "shard"),
         lax.all_to_all(narrow_up, "shard", split_axis=2, concat_axis=1, tiled=True),
     )
     final_down = lax.all_to_all(narrow_down, "shard", split_axis=1, concat_axis=2, tiled=True)

time: 880 us -> 822 us (0.934)
  blocking collectives: 395 us -> 208 us
  waiting for transfers between devices: 251 us -> 405 us
  local copies, waits for them, and re-layouts: 118 us -> 88.9 us
    all_to_all x1 -> x0, blocking collectives: 187 us -> none  [per_device(): lax.all_to_all(narrow_gate, 'shard', split_axis=2, concat_axis=1, tiled=T...]
    all_to_all x1, waiting for transfers between devices: 0.01 us -> 163 us  [per_device(): lax.all_to_all(narrow_down, 'shard', split_axis=1, concat_axis=2, tiled=T...]
    unnamed x22 -> x34, local copies, waits for them, and re-layouts: 67.4 us -> 41.2 us
    all_to_all x1 -> x0, local copies, waits for them, and re-layouts: 12.3 us -> none  [per_device(): lax.all_to_all(narrow_gate, 'shard', split_axis=2, concat_axis=1, tiled=T...]
    pmax x1, waiting for transfers between devices: 92.5 us -> 82.4 us  [per_device(): lax.pmax((jnp.max(jnp.abs(merged_gate), axis=1), jnp.max(jnp.abs(merged_u...]
    convert_element_type x0 -> x1, other arithmetic: none -> 9.39 us  [per_device(): (merged_gate / jnp.expand_dims(scale_gate, 1)).astype(jnp.bfloat16)]
  transfers between devices with their start and end apart: 3 -> 4, of which waited for: 2 -> 3; matrix products, arithmetic and copies ran while one was open for 6% -> 8% of each run, Pallas kernels for 0% -> 0%
where the time goes in v1:
time: 822 us; the launch traced here: 821 us
  waiting for transfers between devices  405 us (49%)
  blocking collectives  208 us (25%)
  other arithmetic  89.9 us (11%)
  local copies, waits for them, and re-layouts  88.9 us (11%)
  starting transfers between devices  15.2 us (2%)
  between operations  14.2 us (2%)
    all_gather x1, blocking collectives, per_device(): row_router = lax.all_gather(part_router, 'shard', axis=0, tiled=True)  202 us
    all_to_all x1, waiting for transfers between devices, per_device(): lax.all_to_all(narrow_down, 'shard', split_axis=1, concat_axis=2, tiled=T...  163 us
    all_to_all x1, waiting for transfers between devices, per_device(): lax.all_to_all(narrow_up, 'shard', split_axis=2, concat_axis=1, tiled=True)  159 us
    pmax x1, waiting for transfers between devices, per_device(): lax.pmax((jnp.max(jnp.abs(merged_gate), axis=1), jnp.max(jnp.abs(merged_u...  82.4 us
    unnamed x34, local copies, waits for them, and re-layouts  41.2 us
    reduce_max x1, other arithmetic, per_device(): jnp.max(jnp.abs(merged_down), axis=2)  30.1 us
    all_to_all x2, local copies, waits for them, and re-layouts, per_device(): lax.all_to_all(narrow_down, 'shard', split_axis=1, concat_axis=2, tiled=T...  24.8 us
    convert_element_type x1, other arithmetic, per_device(): (merged_down / jnp.expand_dims(scale_down, 2)).astype(jnp.bfloat16)  23.8 us
  transfers between devices with their start and end apart: 4, of which 3 were waited for; matrix products, arithmetic and copies ran while one was open for 8% of the time, Pallas kernels for 0%

profile of v1, /device:TPU:0, one launch (start us, length us, event | category | flops | bytes accessed | tf_op | source)
XLA Modules:
  0.0 820.9 jit_solution(3521776614506022651)
XLA Ops:
  7.2 0.0 all-reduce.3.cloned.1.call-start
  7.2 12.5 %copy.28 = bf16[16,256,1024]{1,0,2:T(8,128)(2,1)} copy(bf16[16,256,1024]{2,1,0:T(8,128)(2,1)} %param.11) | data formatting | bytes 16777216 | tf_op args[3]
  19.7 17.6 %copy.29 = f32[16,256,1024]{1,0,2:T(8,128)} copy(f32[16,256,1024]{2,1,0:T(8,128)} %param.10) | data formatting | bytes 33554432 | tf_op args[2]
  37.3 0.0 copy-start
  37.3 10.3 %abs_reduce_fusion.2 = f32[16,1024]{1,0:T(8,128)} fusion(f32[16,256,1024]{2,1,0:T(8,128)} %param.8, bf16[16,256,1024]{2,1,0:T(8,128)(2,1)} %param.9), kind=kLoop, calls=%fused_computation.7 | loop fusion | flops 16760832 | bytes 25231360 | tf_op jit(solution)/shard_map/reduce_max | solution.py:30
  47.6 0.3 copy-done
  47.9 30.1 %abs_reduce_fusion = f32[16,1024]{0,1:T(8,128)} fusion(f32[16,1024,256]{2,1,0:T(8,128)} %param.12, bf16[16,1024,256]{2,1,0:T(8,128)(2,1)S(1)} %copy-done), kind=kLoop, calls=%fused_computation.2 | loop fusion | flops 16760832 | bytes 25231360 | tf_op jit(solution)/shard_map/reduce_max | solution.py:32
  78.0 0.0 slice-done
  78.0 0.0 slice-done.1
  78.0 0.0 slice-done.4
  78.0 0.0 slice-done.2
  78.0 0.0 slice-done.3
  78.1 0.0 slice-done.5
  78.1 4.3 abs_reduce_fusion.1
  82.3 0.0 all-reduce.3.cloned.1.call-update
  82.4 82.4 %all-reduce.3.cloned.1.call-done = (f32[16,1024]{1,0:T(8,128)}, f32[16,1024]{0,1:T(8,128)}, f32[16,1024]{0,1:T(8,128)}) async-done(((f32[16,1024]{1,0:T(8,128)}, f32[16,1024]{0,1:T(8,128)}, f32[16,1024]{0,1:T(8,128)}), (f32[16,1024]{1,0:T(8,128)}, f32[16,1024]{0,1:T(8,128)}, f32[16,1024]{0,1:T(8,128)})) %all-reduce.3.cloned.1.call-update) | async-done | bytes 196624 | tf_op jit(solution)/shard_map/pmax | solution.py:28
  164.8 12.1 %divide_convert_fusion.1 = bf16[16,256,1024]{1,0,2:T(8,128)(2,1)} fusion(f32[16,256,1024]{1,0,2:T(8,128)} %copy.29, bf16[16,256,1024]{1,0,2:T(8,128)(2,1)} %copy.28, f32[16,1024]{0,1:T(8,128)} %get-tuple-element.15), kind=kLoop, calls=%fused_computation.3 | loop fusion | flops 16777216 | bytes 33619968 | tf_op jit(solution)/shard_map/convert_element_type | solution.py:38
  176.9 5.3 all-to-all-start.1
  182.1 0.0 copy-done.1
  182.1 23.8 %divide_convert_fusion = bf16[16,1024,256]{2,0,1:T(8,128)(2,1)} fusion(f32[16,1024,256]{2,1,0:T(8,128)} %param.12, f32[16,1024]{0,1:T(8,128)S(1)} %copy-done.1, bf16[16,1024,256]{2,1,0:T(8,128)(2,1)} %param.13), kind=kLoop, calls=%fused_computation.1 | loop fusion | flops 16777216 | bytes 33619968 | tf_op jit(solution)/shard_map/convert_element_type | solution.py:39
  205.9 159.2 %all-to-all-done.1 = bf16[16,256,1024]{1,0,2:T(8,128)(2,1)} async-done(((bf16[16,256,1024]{1,0,2:T(8,128)(2,1)}), bf16[16,256,1024]{1,0,2:T(8,128)(2,1)}, u32[]{:S(2)}, u32[]{:S(2)}) %all-to-all-start.1) | async-done | bytes 8388640 | tf_op jit(solution)/shard_map/all_to_all | solution.py:43
  365.2 5.0 all-to-all-start.2
  370.1 0.0 copy-done.2
  370.2 9.4 %divide_convert_fusion.2 = bf16[16,256,1024]{2,1,0:T(8,128)(2,1)S(1)} fusion(f32[16,256,1024]{2,1,0:T(8,128)} %param.8, bf16[16,256,1024]{2,1,0:T(8,128)(2,1)} %param.9, f32[16,1024]{1,0:T(8,128)S(1)} %copy-done.2), kind=kLoop, calls=%fused_computation.6 | loop fusion | flops 16777216 | bytes 33619968 | tf_op jit(solution)/shard_map/convert_element_type | solution.py:37
  379.6 1.2 fusion.7
  380.8 1.2 fusion.6
  382.1 1.2 fusion.5
  383.3 1.2 fusion.4
  384.6 1.2 fusion.3
  385.8 1.2 fusion.2
  387.0 1.2 fusion.1
  388.3 1.2 fusion
  389.5 163.0 %all-to-all-done.2 = bf16[16,1024,256]{2,0,1:T(8,128)(2,1)} async-done(((bf16[16,1024,256]{2,0,1:T(8,128)(2,1)}), bf16[16,1024,256]{2,0,1:T(8,128)(2,1)}, u32[]{:S(2)}, u32[]{:S(2)}) %all-to-all-start.2) | async-done | bytes 8388640 | tf_op jit(solution)/shard_map/all_to_all | solution.py:45
  552.6 5.0 all-to-all-start
  557.5 0.0 copy-done.3
  557.6 0.0 copy-done.4
  557.6 202.0 %all_gather.6 = bf16[2048,16]{0,1:T(8,128)(2,1)S(1)} all-gather(bf16[256,16]{0,1:T(8,128)(2,1)S(1)} %multiply_convert_fusion), channel_id=1, replica_groups=mesh['expert'=4,'shard'=8] {'shard'}, dimensions={0}, use_global_device_ids=true | all-gather | bytes 73728 | tf_op jit(solution)/shard_map/all_gather | solution.py:56
  759.5 6.0 all_gather.7
  765.5 0.8 constant_dynamic-slice_fusion
  766.4 0.7 copy.35
  767.1 0.7 copy.34
  767.7 0.6 constant_dynamic-slice_fusion.2
  768.3 12.3 %copy.30 = bf16[16,8,256,128]{3,2,1,0:T(8,128)(2,1)} copy(bf16[16,8,256,128]{2,0,3,1:T(8,128)(2,1)} %bitcast.11) | data formatting | bytes 16777216 | tf_op jit(solution)/shard_map/all_to_all | solution.py:43
  780.6 11.4 %copy.33 = bf16[16,128,8,256]{3,2,1,0:T(8,128)(2,1)} copy(bf16[16,128,8,256]{3,0,1,2:T(8,128)(2,1)} %bitcast.14) | data formatting | bytes 16777216 | tf_op jit(solution)/shard_map/all_to_all | solution.py:45
  792.0 13.4 %all_to_all.37 = bf16[16,128,2048]{2,1,0:T(8,128)(2,1)} reshape(bf16[16,128,8,256]{3,2,1,0:T(8,128)(2,1)} %copy.33) | data formatting | bytes 16777216 | tf_op jit(solution)/shard_map/all_to_all | solution.py:45
  805.4 0.0 all-to-all-done
  805.4 7.9 copy.27
  813.3 0.7 copy.54
  (13 shorter events, 0.0 us)
Async XLA Ops:
  7.2 157.6 %all-reduce.3.cloned.1.call-start = ((), (), s32[]{:S(2)}) async-start(), calls=%async_computation.3 | async-start | bytes 2228224 | tf_op jit(solution)/shard_map/pmax | solution.py:28
  37.3 10.6 %copy-start = (bf16[16,1024,256]{2,1,0:T(8,128)(2,1)S(1)}, bf16[16,1024,256]{2,1,0:T(8,128)(2,1)}, u32[]{:S(2)}) copy-start(bf16[16,1024,256]{2,1,0:T(8,128)(2,1)} %param.13) | copy-start | bytes 25165828
  37.3 40.8 %slice-start = ((s8[16777216]{0:T(1024)(128)(4,1)}), s8[4194304]{0:T(1024)(128)(4,1)S(1)}, s32[]{:S(2)}) async-start(s8[16777216]{0:T(1024)(128)(4,1)} %bitcast.43), calls=%async_computation.4 | async-start | bytes 8388608
  37.3 40.8 %slice-start.1 = ((s8[16777216]{0:T(1024)(128)(4,1)}), s8[4194304]{0:T(1024)(128)(4,1)S(1)}, s32[]{:S(2)}) async-start(s8[16777216]{0:T(1024)(128)(4,1)} %bitcast.43), calls=%async_computation.5 | async-start | bytes 8388608
  37.3 40.8 %slice-start.4 = ((s8[8388608]{0:T(1024)(128)(4,1)}), s8[4194304]{0:T(1024)(128)(4,1)S(1)}, s32[]{:S(2)}) async-start(s8[8388608]{0:T(1024)(128)(4,1)} %bitcast.45), calls=%async_computation.8 | async-start | bytes 8388608
  47.9 30.1 %slice-start.2 = ((s8[16777216]{0:T(1024)(128)(4,1)}), s8[4194304]{0:T(1024)(128)(4,1)S(1)}, s32[]{:S(2)}) async-start(s8[16777216]{0:T(1024)(128)(4,1)} %bitcast.43), calls=%async_computation.6 | async-start | bytes 8388608
  47.9 30.2 %slice-start.3 = ((s8[16777216]{0:T(1024)(128)(4,1)}), s8[4194304]{0:T(1024)(128)(4,1)S(1)}, s32[]{:S(2)}) async-start(s8[16777216]{0:T(1024)(128)(4,1)} %bitcast.43), calls=%async_computation.7 | async-start | bytes 8388608
  47.9 30.2 %slice-start.5 = ((s8[8388608]{0:T(1024)(128)(4,1)}), s8[4194304]{0:T(1024)(128)(4,1)S(1)}, s32[]{:S(2)}) async-start(s8[8388608]{0:T(1024)(128)(4,1)} %bitcast.45), calls=%async_computation.9 | async-start | bytes 8388608
  176.9 5.3 copy-start.1
  176.9 188.3 %all-to-all-start.1 = ((bf16[16,256,1024]{1,0,2:T(8,128)(2,1)}), bf16[16,256,1024]{1,0,2:T(8,128)(2,1)}, u32[]{:S(2)}, u32[]{:S(2)}) async-start(bf16[16,256,1024]{1,0,2:T(8,128)(2,1)} %divide_convert_fusion.1), calls=%async_computation.1 | async-start | bytes 16777216 | tf_op jit(solution)/shard_map/all_to_all | solution.py:43
  205.9 164.2 %copy-start.2 = (f32[16,1024]{1,0:T(8,128)S(1)}, f32[16,1024]{1,0:T(8,128)}, u32[]{:S(2)}) copy-start(f32[16,1024]{1,0:T(8,128)} %get-tuple-element.14) | copy-start | bytes 196612
  365.2 187.4 %all-to-all-start.2 = ((bf16[16,1024,256]{2,0,1:T(8,128)(2,1)}), bf16[16,1024,256]{2,0,1:T(8,128)(2,1)}, u32[]{:S(2)}, u32[]{:S(2)}) async-start(bf16[16,1024,256]{2,0,1:T(8,128)(2,1)} %divide_convert_fusion), calls=%async_computation.2 | async-start | bytes 16777216 | tf_op jit(solution)/shard_map/all_to_all | solution.py:45
  389.5 168.0 %copy-start.3 = (f32[256,16]{0,1:T(8,128)S(1)}, f32[256,16]{0,1:T(8,128)}, u32[]{:S(2)}) copy-start(f32[256,16]{0,1:T(8,128)} %param.14) | copy-start | bytes 49156
  389.5 168.0 %copy-start.4 = (f32[256]{0:T(256)S(1)}, f32[256]{0:T(256)}, u32[]{:S(2)}) copy-start(f32[256]{0:T(256)} %param.15) | copy-start | bytes 3076
  552.6 252.9 %all-to-all-start = ((bf16[8,16,256,128]{3,2,1,0:T(8,128)(2,1)}), bf16[8,16,256,128]{3,2,1,0:T(8,128)(2,1)}, u32[]{:S(2)}, u32[]{:S(2)}) async-start(bf16[8,16,256,128]{3,2,1,0:T(8,128)(2,1)} %fusion), calls=%async_computation | async-start | bytes 16777216 | tf_op jit(solution)/shard_map/all_to_all | solution.py:11
Sparse Core Ops, SparseCore 0:
  82.5 82.2 all-reduce.2
